TPU v7x, 32 devices: a whole 2x2x4 slice. The times are simulated.
32 devices in a mesh: dp: 4 (over y, core), seq: 2 (over x), expert: 4 (over z).
Axes of the slice: x: 2, y: 2, z: 4, core: 2. Of those that a mesh axis runs over, the one named last changes fastest.
Arguments:
- queries: bfloat16 [16, 256, 2560], P(('dp', 'expert'), 'seq'), may hold values from -100 to 100
- key_rows: bfloat16 [16, 256, 512], P(('dp', 'expert'), 'seq'), may hold values from -5 to 5
- value_entries: bfloat16 [16, 256, 512], P(('dp', 'expert'), 'seq'), may hold values from -6 to 6
- features: bfloat16 [4096, 2560], P(('dp', 'seq', 'expert')), may hold values from -0.29882812 to 0.29882812
- router_score: float32 [4096], P(('dp', 'seq', 'expert')), may hold values from -8 to 8
- expert_index: int32 [4096], P(('dp', 'seq', 'expert')), may hold values from 0 to 31, as said below
- slot_index: int32 [4096], P(('dp', 'seq', 'expert')), may hold values from 0 to 35, as said below
- expert_grad: bfloat16 [4608, 2560], P(('dp', 'seq', 'expert')), may hold values from -12 to 12
Outputs:
- attention: bfloat16 [16, 256, 2560], P(('dp', 'expert'), 'seq')
- input_grad: bfloat16 [4096, 2560], P(('dp', 'seq', 'expert'))
- score_grad: float32 [4096], P(('dp', 'seq', 'expert'))
- router_grad: float32 [32, 2560], P('expert', ('dp', 'seq'))
Inputs may be any that keep to these rules, and one draw needn't show every extreme that they name: Among the 128 tokens of one device (aligned blocks, devices in the order dp, seq, expert), at most 36 have one value of expert_index // 8; in every draw some value takes exactly 36 tokens in every block. Tokens of one block with the same expert_index // 8 have different slot_index.
All inputs are finite; a program needn't handle non-finite values.
Results may differ from a plain program's by a relative error of at most 0.0046.
Values may be sent and summed in bfloat16 or wider, within the bound.
No kernel may reach another device: no remote copies, remote signals or barrier semaphores. Data moves between devices by JAX's collectives and lax.ppermute only.
A program may use at most 64 MiB of HBM per device.

v0:
```python
import math

import jax
import jax.numpy as jnp
from jax import lax
from jax.sharding import PartitionSpec as P

HEAD_SIZE = 128
EXP_DEV = 8


def attend_rows(query_part, key_part, value_part, query_start):
    row_count = query_part.shape[0]
    key_count = key_part.shape[0]
    key_heads = key_part.shape[1] // HEAD_SIZE
    group_width = query_part.shape[1] // (key_heads * HEAD_SIZE)
    query_tiles = query_part.reshape(row_count, key_heads, group_width, HEAD_SIZE)
    key_tiles = key_part.reshape(key_count, key_heads, HEAD_SIZE)
    value_tiles = value_part.reshape(key_count, key_heads, HEAD_SIZE)
    scores = jnp.einsum(
        "qkgd,pkd->kgqp", query_tiles, key_tiles, preferred_element_type=jnp.float32
    ) * (1.0 / math.sqrt(HEAD_SIZE))
    query_pos = query_start + lax.broadcasted_iota(jnp.int32, (row_count, key_count), 0)
    key_pos = lax.broadcasted_iota(jnp.int32, (row_count, key_count), 1)
    scores = jnp.where(query_pos >= key_pos, scores, -jnp.inf)
    row_max = jnp.max(scores, axis=-1, keepdims=True)
    exp_scores = jnp.exp(scores - row_max)
    weights = (exp_scores / jnp.sum(exp_scores, axis=-1, keepdims=True)).astype(jnp.bfloat16)
    mixed_out = jnp.einsum(
        "kgqp,pkd->qkgd", weights, value_tiles, preferred_element_type=jnp.float32
    )
    return mixed_out.reshape(row_count, key_heads * group_width * HEAD_SIZE).astype(jnp.bfloat16)


def attend_all(query_part, key_part, value_part, query_start):
    return attend_rows(query_part, key_part, value_part, query_start)


def local(
    queries, key_rows, value_entries, features, router_score, expert_index, slot_index, expert_grad
):
    key_all, value_all = (
        lax.all_gather(key_rows, "seq", axis=1, tiled=True),
        lax.all_gather(value_entries, "seq", axis=1, tiled=True),
    )
    offset = lax.axis_index("seq") * queries.shape[1]
    attention = jax.vmap(
        lambda query_one, key_one, value_one: attend_all(query_one, key_one, value_one, offset)
    )(queries, key_all, value_all)
    expert_count = lax.axis_size("expert")
    capacity = expert_grad.shape[0] // expert_count
    feature_width = features.shape[1]
    token_count = features.shape[0]
    returned = lax.all_to_all(
        expert_grad.reshape(expert_count, capacity, feature_width),
        "expert",
        split_axis=0,
        concat_axis=0,
        tiled=True,
    )
    returned = returned.reshape(expert_count * capacity, feature_width)
    target = expert_index // EXP_DEV
    slot_cell = target * capacity + slot_index
    cell_grid = lax.broadcasted_iota(jnp.int32, (token_count, expert_count * capacity), 1)
    picker = (slot_cell[:, None] == cell_grid).astype(jnp.bfloat16)
    routed = jnp.dot(picker, returned, preferred_element_type=jnp.float32)
    gate_value = jax.nn.sigmoid(router_score)
    input_grad = (gate_value[:, None] * routed).astype(jnp.bfloat16)
    feature_wide = features.astype(jnp.float32)
    inner_sum = jnp.sum(routed * feature_wide, axis=1)
    score_grad = inner_sum * gate_value * (1.0 - gate_value)
    experts_all = EXP_DEV * expert_count
    column_grid = lax.broadcasted_iota(jnp.int32, (token_count, experts_all), 1)
    weighted = jnp.where(
        expert_index[:, None] == column_grid, score_grad[:, None], jnp.zeros((), jnp.float32)
    )
    per_expert = lax.psum_scatter(
        jnp.dot(weighted.T, feature_wide, precision=lax.Precision.HIGHEST),
        "expert",
        scatter_dimension=0,
        tiled=True,
    )
    router_grad = lax.psum_scatter(per_expert, ("dp", "seq"), scatter_dimension=1, tiled=True)
    return (attention, input_grad, score_grad, router_grad)


def solution(mesh):
    placed = (
        P(("dp", "expert"), "seq", None),
        P(("dp", "expert"), "seq", None),
        P(("dp", "expert"), "seq", None),
        P(("dp", "seq", "expert"), None),
        P(("dp", "seq", "expert")),
        P(("dp", "seq", "expert")),
        P(("dp", "seq", "expert")),
        P(("dp", "seq", "expert"), None),
    )
    return jax.shard_map(
        local,
        mesh=mesh,
        in_specs=placed,
        out_specs=(
            P(("dp", "expert"), "seq", None),
            P(("dp", "seq", "expert"), None),
            P(("dp", "seq", "expert")),
            P("expert", ("dp", "seq")),
        ),
        check_vma=False,
    )
```

profile of v0, /device:TPU:0, one launch (start us, length us, event | category | flops | bytes accessed | tf_op | source)
XLA Modules:
  0.0 108.8 jit_solution(13287607287325676137)
XLA Ops:
  7.2 2.2 %reshape.69 = bf16[4,36,2560]{2,1,0:T(8,128)(2,1)} reshape(bf16[144,2560]{1,0:T(8,128)(2,1)} %param.15) | data formatting | bytes 1474560 | tf_op jit(solution)/shard_map/reshape | solution.py:55
  9.4 6.5 %all-to-all-start = ((bf16[4,36,2560]{2,1,0:T(8,128)(2,1)}), bf16[4,36,2560]{2,1,0:T(8,128)(2,1)S(1)}, u32[]{:S(2)}, u32[]{:S(2)}) async-start(bf16[4,36,2560]{2,1,0:T(8,128)(2,1)} %reshape.69), calls=%async_computation | async-start | bytes 1638400 | tf_op jit(solution)/shard_map/all_to_all | solution.py:54
  15.9 1.1 copy.24
  17.0 0.1 copy.23
  17.1 5.6 %all_gather.7 = bf16[1,256,512]{2,1,0:T(8,128)(2,1)S(1)} all-gather(bf16[1,128,512]{2,1,0:T(8,128)(2,1)S(1)} %copy-done.3), channel_id=1, replica_groups=mesh['dp'=4,'seq'=2,'expert'=4] {'seq'}, dimensions={1}, use_global_device_ids=true | all-gather | bytes 393216 | tf_op jit(solution)/shard_map/all_gather | solution.py:44
  22.8 0.8 copy.27
  23.6 5.7 %all_gather.6 = bf16[1,256,512]{1,2,0:T(8,128)(2,1)S(1)} all-gather(bf16[1,128,512]{1,2,0:T(8,128)(2,1)S(1)} %copy.23), channel_id=1, replica_groups=mesh['dp'=4,'seq'=2,'expert'=4] {'seq'}, dimensions={1}, use_global_device_ids=true | all-gather | bytes 393216 | tf_op jit(solution)/shard_map/all_gather | solution.py:43
  29.3 1.7 %fusion.1 = (f32[4,5,128]{2,1,0:T(8,128)S(1)}, f32[4,256,128,5]{2,1,3,0:T(8,128)S(1)}) fusion(pred[128,256]{0,1:T(8,128)(4,1)S(1)} %iota_compare_fusion.1, bf16[256,4,128,1]{0,2,3,1:T(8,128)(2,1)S(1)} %bitcast.43, bf16[128,4,5,128]{0,3,2,1:T(8,128)(2,1)} %bitcast.42), kind=kOutput, calls=%fused_computation.4 | convolution fusion | flops 169735680 | bytes 3581952 | tf_op jit(solution)/shard_map/vmap(qkgd,pkd->kgqp)/dot_general | solution.py:20
  31.0 5.7 %all-to-all-done = bf16[4,36,2560]{2,1,0:T(8,128)(2,1)S(1)} async-done(((bf16[4,36,2560]{2,1,0:T(8,128)(2,1)}), bf16[4,36,2560]{2,1,0:T(8,128)(2,1)S(1)}, u32[]{:S(2)}, u32[]{:S(2)}) %all-to-all-start) | async-done | bytes 737312 | tf_op jit(solution)/shard_map/all_to_all | solution.py:54
  36.7 1.0 reshape.70
  37.8 2.8 %multiply_reduce_fusion = (f32[128]{0:T(128)S(1)}, f32[128,2560]{1,0:T(8,128)}) fusion(bf16[128,2560]{1,0:T(8,128)(2,1)} %param.11, bf16[144,2560]{1,0:T(8,128)(2,1)} %reshape.70, s32[128]{0:T(128)S(1)} %multiply_add_fusion), kind=kOutput, calls=%fused_computation.7 | convolution fusion | flops 95373184 | bytes 2704384 | tf_op jit(solution)/shard_map/dot_general | solution.py:66
  40.6 0.0 copy-start.5
  40.6 1.2 %fusion.5 = f32[32,2560]{1,0:T(8,128)} fusion(bf16[128,2560]{1,0:T(8,128)(2,1)S(1)} %copy-done.1, f32[128]{0:T(128)S(1)} %get-tuple-element.16, s32[128]{0:T(128)S(1)} %copy-done.6), kind=kOutput, calls=%fused_computation.13 | convolution fusion | flops 125837312 | bytes 984064 | tf_op jit(solution)/shard_map/dot_general | solution.py:78
  41.9 0.0 reduce-scatter.5.cloned.1.call-update
  41.9 0.0 reduce-scatter.7.cloned.1.call-start
  41.9 0.5 fusion
  42.5 1.8 %convolution_convert_fusion = bf16[4,5,128,128]{2,3,1,0:T(8,128)(2,1)S(1)} fusion(bf16[256,4,128,1]{0,2,3,1:T(8,128)(2,1)} %bitcast.45, f32[4,256,128,5]{2,1,3,0:T(8,128)S(1)} %get-tuple-element.19, f32[4,5,128]{2,1,0:T(8,128)S(1)} %fusion, f32[4,5,128]{2,1,0:T(8,128)S(1)} %get-tuple-element.18, pred[128,256]{0,1:T(8,128)(4,1)S(1)} %iota_compare_fusion.1), kind=kOutput, calls=%fused_computation.5 | convolution fusion | flops 171376640 | bytes 3592192 | tf_op jit(solution)/shard_map/vmap(kgqp,pkd->qkgd)/dot_general | solution.py:29
  44.3 1.1 copy.29
  45.4 16.2 %reduce-scatter.5.cloned.1.call-done = f32[8,2560]{1,0:T(8,128)} async-done(((f32[32,2560]{1,0:T(8,128)}), f32[8,2560]{1,0:T(8,128)}) %reduce-scatter.5.cloned.1.call-update) | async-done | bytes 81936 | tf_op jit(solution)/shard_map/reduce_scatter | solution.py:77
  61.6 2.4 %copy.36 = f32[8,2560]{0,1:T(8,128)} copy(f32[8,2560]{1,0:T(8,128)} %reduce-scatter.5.cloned.1.call-done) | data formatting | bytes 163840
  64.0 0.0 reduce-scatter.7.cloned.1.call-update
  64.0 1.0 multiply_convert_fusion
  65.0 35.3 %reduce-scatter.7.cloned.1.call-done = f32[320,8]{1,0:T(8,128)} async-done(((f32[2560,8]{1,0:T(8,128)}), f32[320,8]{1,0:T(8,128)}) %reduce-scatter.7.cloned.1.call-update) | async-done | bytes 10256
  100.4 1.6 %copy.37 = f32[8,320]{1,0:T(8,128)} copy(f32[8,320]{0,1:T(8,128)} %bitcast.46) | data formatting | bytes 20480
  (22 shorter events, 0.1 us)
Async XLA Ops:
  7.2 8.8 %copy-start.2 = (bf16[1,128,2560]{2,1,0:T(8,128)(2,1)S(1)}, bf16[1,128,2560]{2,1,0:T(8,128)(2,1)}, u32[]{:S(2)}) copy-start(bf16[1,128,2560]{2,1,0:T(8,128)(2,1)} %param.8) | copy-start | bytes 1966084
  7.2 9.8 %copy-start.4 = (bf16[1,128,512]{2,1,0:T(8,128)(2,1)S(1)}, bf16[1,128,512]{2,1,0:T(8,128)(2,1)}, u32[]{:S(2)}) copy-start(bf16[1,128,512]{2,1,0:T(8,128)(2,1)} %param.9) | copy-start | bytes 393220
  7.2 9.9 %copy-start.3 = (bf16[1,128,512]{2,1,0:T(8,128)(2,1)S(1)}, bf16[1,128,512]{2,1,0:T(8,128)(2,1)}, u32[]{:S(2)}) copy-start(bf16[1,128,512]{2,1,0:T(8,128)(2,1)} %param.10) | copy-start | bytes 393220
  9.4 19.8 %copy-start.6 = (s32[128]{0:T(128)S(1)}, s32[128]{0:T(128)}, u32[]{:S(2)}) copy-start(s32[128]{0:T(128)} %param.13) | copy-start | bytes 1540
  9.4 19.8 %copy-start.8 = (s32[128]{0:T(128)S(1)}, s32[128]{0:T(128)}, u32[]{:S(2)}) copy-start(s32[128]{0:T(128)} %param.14) | copy-start | bytes 1540
  9.4 27.3 %all-to-all-start = ((bf16[4,36,2560]{2,1,0:T(8,128)(2,1)}), bf16[4,36,2560]{2,1,0:T(8,128)(2,1)S(1)}, u32[]{:S(2)}, u32[]{:S(2)}) async-start(bf16[4,36,2560]{2,1,0:T(8,128)(2,1)} %reshape.69), calls=%async_computation | async-start | bytes 1638400 | tf_op jit(solution)/shard_map/all_to_all | solution.py:54
  15.9 45.7 %reduce-scatter.5.cloned.1.call-start = ((), (), s32[]{:S(2)}) async-start(), calls=%async_computation.3 | async-start | bytes 409600 | tf_op jit(solution)/shard_map/reduce_scatter | solution.py:77
  31.0 9.6 %copy-start.7 = (f32[128]{0:T(128)S(1)}, f32[128]{0:T(128)}, u32[]{:S(2)}) copy-start(f32[128]{0:T(128)} %param.12) | copy-start | bytes 1540
  37.8 2.9 %copy-start.1 = (bf16[128,2560]{1,0:T(8,128)(2,1)S(1)}, bf16[128,2560]{1,0:T(8,128)(2,1)}, u32[]{:S(2)}) copy-start(bf16[128,2560]{1,0:T(8,128)(2,1)} %param.11) | copy-start | bytes 1966084
  40.6 3.7 %copy-start.5 = (f32[128]{0:T(128)}, f32[128]{0:T(128)S(1)}, u32[]{:S(2)}) copy-start(f32[128]{0:T(128)S(1)} %get-tuple-element.16) | copy-start | bytes 1540
  41.9 58.5 %reduce-scatter.7.cloned.1.call-start = ((), (), s32[]{:S(2)}) async-start(), calls=%async_computation.4 | async-start | bytes 1474560
  44.3 19.7 %copy-start = (f32[128,2560]{1,0:T(8,128)S(1)}, f32[128,2560]{1,0:T(8,128)}, u32[]{:S(2)}) copy-start(f32[128,2560]{1,0:T(8,128)} %get-tuple-element.21) | copy-start | bytes 3932164
Sparse Core Ops, SparseCore 0:
  42.0 19.5 reduce-scatter.4
  64.9 35.4 reduce-scatter.6
where the time goes:
time: 109 us
  waiting for transfers between devices  57.3 us (53%)
  between operations  14.2 us (13%)
  blocking collectives  11.3 us (10%)
  local copies, waits for them, and re-layouts  10.4 us (10%)
  matrix products  7.54 us (7%)
  starting transfers between devices  6.52 us (6%)
  other arithmetic  1.57 us (1%)
    unnamed x3, waiting for transfers between devices  35.4 us
    reduce_scatter x1, waiting for transfers between devices, local(): lax.psum_scatter(jnp.dot(weighted.T, feature_wide, precision=lax.Precisio...  16.2 us
    all_to_all x1, starting transfers between devices, local(): lax.all_to_all(expert_grad.reshape(expert_count, capacity, feature_width)...  6.48 us
    unnamed x23, local copies, waits for them, and re-layouts  6.3 us
    all_to_all x1, waiting for transfers between devices, local(): lax.all_to_all(expert_grad.reshape(expert_count, capacity, feature_width)...  5.73 us
    all_gather x1, blocking collectives, local(): lax.all_gather(key_rows, 'seq', axis=1, tiled=True)  5.65 us
    all_gather x1, blocking collectives, local(): lax.all_gather(value_entries, 'seq', axis=1, tiled=True)  5.64 us
    dot_general x1, matrix products, local(): routed = jnp.dot(picker, returned, preferred_element_type=jnp.float32)  2.82 us
  transfers between devices with their start and end apart: 3, of which 3 were waited for; matrix products, arithmetic and copies ran while one was open for 7% of the time, Pallas kernels for 0%

commit v1 on v0

v1 whole, which is shorter than its diff:
```python
import functools
import math

import jax
import jax.numpy as jnp
from jax import lax
from jax.experimental import pallas as pl
from jax.experimental.pallas import tpu as pltpu
from jax.sharding import PartitionSpec as P

HEAD_SIZE = 128
EXP_DEV = 8
DIRECT_LIMIT = 64


def round_up(value, step):
    return (value + step - 1) // step * step


def is_power(value):
    return value & (value - 1) == 0


def partner_pairs(count, step):
    if is_power(count):
        return [(i, i ^ step) for i in range(count)]
    return [(i, (i + step) % count) for i in range(count)]


def block_to_send(me, count, step):
    return me ^ step if is_power(count) else lax.rem(me + step, count)


def source_step(me, count, source):
    if is_power(count):
        return me ^ source
    return lax.rem(me - source + count, count)


def whole_vmem():
    return pl.BlockSpec(memory_space=pltpu.VMEM)


def attention_kernel(seq_count, q_ref, *refs):
    kv_refs, out_ref = refs[:-1], refs[-1]
    head_group = q_ref.shape[2] // HEAD_SIZE
    rows = q_ref.shape[1]
    me = lax.axis_index("seq")
    scale = 1.0 / math.sqrt(HEAD_SIZE)
    lower = lax.broadcasted_iota(jnp.int32, (rows, rows), 0) >= lax.broadcasted_iota(
        jnp.int32, (rows, rows), 1
    )
    keys = [kv_refs[2 * b] for b in range(seq_count)]
    values = [kv_refs[2 * b + 1] for b in range(seq_count)]
    for head in range(head_group):
        span = slice(head * HEAD_SIZE, (head + 1) * HEAD_SIZE)
        query = q_ref[0, :, span]
        tiles = []
        for b in range(seq_count):
            tile = (
                lax.dot_general(
                    query,
                    keys[b][0],
                    (((1,), (1,)), ((), ())),
                    preferred_element_type=jnp.float32,
                )
                * scale
            )
            if b == 0:
                tile = jnp.where(lower, tile, -jnp.inf)
            else:
                tile = jnp.where(lax.rem(me + seq_count - b, seq_count) < me, tile, -jnp.inf)
            tiles.append(tile)
        top = jnp.max(functools.reduce(jnp.maximum, tiles), axis=1, keepdims=True)
        weights = [jnp.exp(tile - top) for tile in tiles]
        total = jnp.sum(functools.reduce(jnp.add, weights), axis=1, keepdims=True)
        mixed = None
        for b in range(seq_count):
            term = jnp.dot(
                weights[b].astype(jnp.bfloat16), values[b][0], preferred_element_type=jnp.float32
            )
            mixed = term if mixed is None else mixed + term
        out_ref[0, :, span] = (mixed / total).astype(jnp.bfloat16)


def attend(queries, key_rows, value_entries):
    seq_count = lax.axis_size("seq")
    batch, rows, width = queries.shape
    kv_heads = key_rows.shape[2] // HEAD_SIZE
    group_columns = width // kv_heads
    key_value = jnp.concatenate([key_rows, value_entries], axis=2)
    operands = [key_rows, value_entries]
    kv_block = (1, rows, HEAD_SIZE)
    specs = [pl.BlockSpec(kv_block, lambda s, h: (s, 0, h))] * 2
    for step in range(1, seq_count):
        pairs = [(i, (i + step) % seq_count) for i in range(seq_count)]
        other = lax.ppermute(key_value, "seq", pairs)
        operands += [other, other]
        specs += [
            pl.BlockSpec(kv_block, lambda s, h: (s, 0, h)),
            pl.BlockSpec(kv_block, lambda s, h: (s, 0, kv_heads + h)),
        ]
    q_spec = pl.BlockSpec((1, rows, group_columns), lambda s, h: (s, 0, h))
    return pl.pallas_call(
        functools.partial(attention_kernel, seq_count),
        grid=(batch, kv_heads),
        in_specs=[q_spec] + specs,
        out_specs=q_spec,
        out_shape=jax.ShapeDtypeStruct(queries.shape, jnp.bfloat16),
        compiler_params=pltpu.CompilerParams(vmem_limit_bytes=16 * 2**20),
        cost_estimate=pl.CostEstimate(
            flops=4 * batch * rows * rows * seq_count * width,
            bytes_accessed=4 * batch * rows * width,
            transcendentals=batch * rows * rows * seq_count * width // HEAD_SIZE,
        ),
        name="attend",
    )(queries, *operands)


def token_cells(count, padded, expert_row, slot_row):
    me = lax.axis_index("expert")
    target = lax.shift_right_logical(expert_row, EXP_DEV.bit_length() - 1)
    return source_step(me, count, target) * padded + slot_row


def slot_kernel(count, padded, expert_ref, slot_ref, score_ref, feature_ref, moved_ref, weight_ref):
    tokens = feature_ref.shape[0]
    cells, experts = weight_ref.shape
    cell_row = token_cells(count, padded, expert_ref[...], slot_ref[...])
    chosen = lax.broadcasted_iota(jnp.int32, (cells, tokens), 0) == cell_row
    gate = 1.0 / (1.0 + jnp.exp(-score_ref[...]))
    slope = jnp.sum(jnp.where(chosen, gate * (1.0 - gate), 0.0), axis=1, keepdims=True)
    owner = jnp.sum(
        jnp.where(chosen, expert_ref[...].astype(jnp.float32), 0.0), axis=1, keepdims=True
    )
    columns = lax.broadcasted_iota(jnp.int32, (cells, experts), 1).astype(jnp.float32)
    weight_ref[...] = jnp.where(owner == columns, slope, 0.0)
    picker = jnp.where(chosen, 1.0, 0.0).astype(jnp.bfloat16)
    moved_ref[...] = jnp.dot(
        picker, feature_ref[...], preferred_element_type=jnp.float32
    ).astype(jnp.bfloat16)


def partial_kernel(count, padded, slab, *refs):
    chunk_refs = refs[:count]
    moved_ref, weight_ref, out_ref, inner_ref = refs[count:]
    cells, experts = weight_ref.shape
    capacity, width = chunk_refs[0].shape
    inner_ref[...] = jnp.zeros_like(inner_ref)
    for k in range(count):
        span = slice(k * padded, k * padded + capacity)
        inner_ref[span, :] = jnp.sum(
            chunk_refs[k][...].astype(jnp.float32) * moved_ref[span, :].astype(jnp.float32),
            axis=1,
            keepdims=True,
        )
    weighted = weight_ref[...] * inner_ref[...]
    high = weighted.astype(jnp.bfloat16)
    low = (weighted - high.astype(jnp.float32)).astype(jnp.bfloat16)
    both = lax.dot_general(
        jnp.concatenate([high, low], axis=1),
        moved_ref[...],
        (((0,), (0,)), ((), ())),
        preferred_element_type=jnp.float32,
    )
    sums = both[:experts] + both[experts:]
    if slab is None:
        out_ref[...] = sums
        return
    rolled = pltpu.roll(sums, width - slab % HEAD_SIZE, 1) if slab % HEAD_SIZE else sums
    groups = experts // EXP_DEV
    for c in range(width // slab):
        start = c * slab
        source = sums
        if start % HEAD_SIZE:
            source, start = rolled, start - slab % HEAD_SIZE
        for e in range(groups):
            out_ref[c * groups + e] = source[
                e * EXP_DEV : (e + 1) * EXP_DEV, start : start + slab
            ].astype(jnp.bfloat16)


def output_kernel(count, padded, expert_ref, slot_ref, score_ref, inner_ref, *refs):
    chunk_refs = refs[:count]
    input_ref, score_out_ref = refs[count:]
    tokens = input_ref.shape[0]
    capacity = chunk_refs[0].shape[0]
    cells = inner_ref.shape[0]
    cell_row = token_cells(count, padded, expert_ref[...], slot_ref[...])
    chosen = lax.broadcasted_iota(jnp.int32, (cells, tokens), 0) == cell_row
    gate = 1.0 / (1.0 + jnp.exp(-score_ref[...]))
    inner = jnp.sum(jnp.where(chosen, inner_ref[...], 0.0), axis=0, keepdims=True)
    score_out_ref[...] = inner * gate * (1.0 - gate)
    square = lax.broadcasted_iota(jnp.int32, (tokens, tokens), 0) == lax.broadcasted_iota(
        jnp.int32, (tokens, tokens), 1
    )
    gate_column = jnp.sum(jnp.where(square, gate, 0.0), axis=1, keepdims=True)
    picker = jnp.where(chosen, 1.0, 0.0)
    routed = None
    for k in range(count):
        part = picker[k * padded : k * padded + capacity].astype(jnp.bfloat16)
        term = lax.dot_general(
            part, chunk_refs[k][...], (((0,), (0,)), ((), ())), preferred_element_type=jnp.float32
        )
        routed = term if routed is None else routed + term
    input_ref[...] = (gate_column * routed).astype(jnp.bfloat16)


def local(
    queries, key_rows, value_entries, features, router_score, expert_index, slot_index, expert_grad
):
    count = lax.axis_size("expert")
    me = lax.axis_index("expert")
    slabs = lax.axis_size("dp") * lax.axis_size("seq")
    capacity = expert_grad.shape[0] // count
    padded = round_up(capacity, 8)
    tokens, width = features.shape
    experts = EXP_DEV * count
    cells = count * padded
    blocks = expert_grad.reshape(count, capacity, width)

    chunks = [lax.dynamic_index_in_dim(blocks, me, 0, keepdims=False)] + [None] * (count - 1)
    for step in range(count - 1, 0, -1):
        piece = lax.dynamic_index_in_dim(
            blocks, block_to_send(me, count, step), 0, keepdims=False
        )
        chunks[step] = lax.ppermute(piece, "expert", partner_pairs(count, step))

    attention = attend(queries, key_rows, value_entries)

    expert_row = expert_index.reshape(1, tokens)
    slot_row = slot_index.reshape(1, tokens)
    score_row = router_score.reshape(1, tokens)
    small = pltpu.CompilerParams(vmem_limit_bytes=16 * 2**20)
    moved, weight = pl.pallas_call(
        functools.partial(slot_kernel, count, padded),
        in_specs=[whole_vmem()] * 4,
        out_specs=[whole_vmem()] * 2,
        out_shape=[
            jax.ShapeDtypeStruct((cells, width), jnp.bfloat16),
            jax.ShapeDtypeStruct((cells, experts), jnp.float32),
        ],
        compiler_params=small,
        cost_estimate=pl.CostEstimate(
            flops=2 * cells * tokens * width, bytes_accessed=4 * tokens * width, transcendentals=0
        ),
        name="to_slots",
    )(expert_row, slot_row, score_row, features)

    slab = width // slabs
    direct = slabs * count <= DIRECT_LIMIT and slab % (HEAD_SIZE // 2) == 0
    sums_shape = (
        jax.ShapeDtypeStruct((slabs * count, EXP_DEV, slab), jnp.bfloat16)
        if direct
        else jax.ShapeDtypeStruct((experts, width), jnp.float32)
    )
    sums, inner = pl.pallas_call(
        functools.partial(partial_kernel, count, padded, slab if direct else None),
        in_specs=[whole_vmem()] * (count + 2),
        out_specs=[whole_vmem()] * 2,
        out_shape=[sums_shape, jax.ShapeDtypeStruct((cells, 1), jnp.float32)],
        compiler_params=small,
        cost_estimate=pl.CostEstimate(
            flops=4 * cells * experts * width, bytes_accessed=2 * cells * width, transcendentals=0
        ),
        name="partial_sums",
    )(*chunks, moved, weight)
    if direct:
        parts = lax.all_to_all(
            sums, ("dp", "seq", "expert"), split_axis=0, concat_axis=0, tiled=True
        )
        router_grad = jnp.sum(parts.astype(jnp.float32), axis=0)
    else:
        per_expert = lax.psum_scatter(sums, "expert", scatter_dimension=0, tiled=True)
        router_grad = lax.psum_scatter(per_expert, ("dp", "seq"), scatter_dimension=1, tiled=True)

    input_grad, score_grad = pl.pallas_call(
        functools.partial(output_kernel, count, padded),
        in_specs=[whole_vmem()] * (count + 4),
        out_specs=[whole_vmem()] * 2,
        out_shape=[
            jax.ShapeDtypeStruct((tokens, width), jnp.bfloat16),
            jax.ShapeDtypeStruct((1, tokens), jnp.float32),
        ],
        compiler_params=small,
        cost_estimate=pl.CostEstimate(
            flops=2 * cells * tokens * width, bytes_accessed=4 * tokens * width, transcendentals=0
        ),
        name="token_outputs",
    )(expert_row, slot_row, score_row, inner, *chunks)
    return (attention, input_grad, score_grad.reshape(tokens), router_grad)


def solution(mesh):
    tokens_spec = P(("dp", "seq", "expert"))
    rows_spec = P(("dp", "seq", "expert"), None)
    sequence_spec = P(("dp", "expert"), "seq", None)
    return jax.shard_map(
        local,
        mesh=mesh,
        in_specs=(
            sequence_spec,
            sequence_spec,
            sequence_spec,
            rows_spec,
            tokens_spec,
            tokens_spec,
            tokens_spec,
            rows_spec,
        ),
        out_specs=(sequence_spec, rows_spec, tokens_spec, P("expert", ("dp", "seq"))),
        check_vma=False,
    )
```

time: 109 us -> 49.3 us (0.45)
  waiting for transfers between devices: 57.3 us -> 20.9 us
  between operations: 14.2 us -> 0.74 us
  blocking collectives: 11.3 us -> 0 us
  Pallas kernels: 0 us -> 10.3 us
  local copies, waits for them, and re-layouts: 10.4 us -> 2.05 us
  starting transfers between devices: 6.52 us -> 14.4 us
  matrix products: 7.54 us -> 0 us
    unnamed x3 -> x0, waiting for transfers between devices: 35.4 us -> none
    ppermute x0 -> x4, waiting for transfers between devices: none -> 20.9 us  [the longest x3 14 us: local(): chunks[step] = lax.ppermute(piece, 'expert', partner_pairs(count, step))]
    reduce_scatter x1 -> x0, waiting for transfers between devices: 16.2 us -> none  [local(): lax.psum_scatter(jnp.dot(weighted.T, feature_wide, precision=lax.Precisio...]
    all_gather x2 -> x0, blocking collectives: 11.3 us -> none  [the longest x1 5.65 us: local(): lax.all_gather(key_rows, 'seq', axis=1, tiled=True)]
    pallas_call x0 -> x4, Pallas kernels: none -> 10.3 us  [the longest x1 6.72 us: attend(): pl.pallas_call(functools.partial(attention_kernel, seq_count), grid=(batc...]
    ppermute x0 -> x4, starting transfers between devices: none -> 7.54 us  [the longest x3 5.71 us: local(): chunks[step] = lax.ppermute(piece, 'expert', partner_pairs(count, step))]
    dot_general x4 -> x0, matrix products: 7.54 us -> none  [the longest x1 2.82 us: local(): routed = jnp.dot(picker, returned, preferred_element_type=jnp.float32)]
    all_to_all x1, waiting for transfers between devices: 5.73 us -> 0.01 us  [local(): lax.all_to_all(sums, ('dp', 'seq', 'expert'), split_axis=0, concat_axis=0...]
  transfers between devices with their start and end apart: 3 -> 5, of which waited for: 3 -> 3; matrix products, arithmetic and copies ran while one was open for 7% -> 0% of each run, Pallas kernels for 0% -> 18%
where the time goes in v1:
time: 49.3 us; the launch traced here: 49.1 us
  waiting for transfers between devices  20.9 us (42%)
  starting transfers between devices  14.4 us (29%)
  Pallas kernels  10.3 us (21%)
  local copies, waits for them, and re-layouts  2.05 us (4%)
  between operations  0.74 us (2%)
  other arithmetic  0.66 us (1%)
    ppermute x3, waiting for transfers between devices, local(): chunks[step] = lax.ppermute(piece, 'expert', partner_pairs(count, step))  14 us
    ppermute x1, waiting for transfers between devices, attend(): other = lax.ppermute(key_value, 'seq', pairs)  6.92 us
    all_to_all x1, starting transfers between devices, local(): lax.all_to_all(sums, ('dp', 'seq', 'expert'), split_axis=0, concat_axis=0...  6.85 us
    pallas_call x1, Pallas kernels, attend(): pl.pallas_call(functools.partial(attention_kernel, seq_count), grid=(batc...  6.72 us
    ppermute x3, starting transfers between devices, local(): chunks[step] = lax.ppermute(piece, 'expert', partner_pairs(count, step))  5.71 us
    ppermute x1, starting transfers between devices, attend(): other = lax.ppermute(key_value, 'seq', pairs)  1.83 us
    pallas_call x1, Pallas kernels, local(): pl.pallas_call(functools.partial(output_kernel, count, padded), in_specs=...  1.75 us
    pallas_call x1, Pallas kernels, local(): pl.pallas_call(functools.partial(partial_kernel, count, padded, slab if d...  1.52 us
  transfers between devices with their start and end apart: 5, of which 3 were waited for; matrix products, arithmetic and copies ran while one was open for 0% of the time, Pallas kernels for 18%

profile of v1, /device:TPU:0, one launch (start us, length us, event | category | flops | bytes accessed | tf_op | source)
XLA Modules:
  0.0 49.1 jit_solution(15177784275655713050)
XLA Ops:
  0.6 1.3 %reshape.26 = bf16[4,36,2560]{2,1,0:T(8,128)(2,1)S(1)} reshape(bf16[144,2560]{1,0:T(8,128)(2,1)} %param.15) | data formatting | bytes 1474560 | tf_op jit(solution)/shard_map/reshape | solution.py:220
  1.9 0.0 copy-start
  1.9 0.1 dynamic-slice_bitcast_fusion
  2.0 3.1 %collective-permute-start.1 = (bf16[36,2560]{1,0:T(8,128)(2,1)S(1)}, bf16[36,2560]{1,0:T(8,128)(2,1)S(1)}, u32[]{:S(2)}, u32[]{:S(2)}) collective-permute-start(bf16[36,2560]{1,0:T(8,128)(2,1)S(1)} %get-tuple-element.18), channel_id=1, source_target_pairs={{0,1},{1,0},{2,3},{3,2},{4,5},{5,4},{6,7},{7,6},{8,9},{9,8},{10,11... | collective-permute-start | bytes 552968 | tf_op jit(solution)/shard_map/ppermute | solution.py:227
  5.2 2.6 %collective-permute-start.2 = (bf16[36,2560]{1,0:T(8,128)(2,1)S(1)}, bf16[36,2560]{1,0:T(8,128)(2,1)S(1)}, u32[]{:S(2)}, u32[]{:S(2)}) collective-permute-start(bf16[36,2560]{1,0:T(8,128)(2,1)S(1)} %get-tuple-element.17), channel_id=1, source_target_pairs={{0,2},{1,3},{2,0},{3,1},{4,6},{5,7},{6,4},{7,5},{8,10},{9,11},{10,... | collective-permute-start | bytes 552968 | tf_op jit(solution)/shard_map/ppermute | solution.py:227
  7.7 0.0 collective-permute-start.3
  7.8 0.0 copy-done
  7.8 0.6 %copy-done.4 = s32[128]{0:T(128)S(1)} copy-done((s32[128]{0:T(128)S(1)}, s32[128]{0:T(128)}, u32[]{:S(2)}) %copy-start.4) | copy-done | bytes 536
  8.4 0.0 copy-done.5
  8.4 0.0 copy-done.6
  8.4 0.4 to_slots.1
  8.8 5.1 %collective-permute-done.1.refs_1_ = bf16[36,2560]{1,0:T(8,128)(2,1)S(1)} collective-permute-done((bf16[36,2560]{1,0:T(8,128)(2,1)S(1)}, bf16[36,2560]{1,0:T(8,128)(2,1)S(1)}, u32[]{:S(2)}, u32[]{:S(2)}) %collective-permute-start.1) | collective-permute-done | bytes 184352 | tf_op jit(solution)/shard_map/ppermute | solution.py:227
  13.9 8.9 %collective-permute-done.2.refs_2_ = bf16[36,2560]{1,0:T(8,128)(2,1)S(1)} collective-permute-done((bf16[36,2560]{1,0:T(8,128)(2,1)S(1)}, bf16[36,2560]{1,0:T(8,128)(2,1)S(1)}, u32[]{:S(2)}, u32[]{:S(2)}) %collective-permute-start.2) | collective-permute-done | bytes 184352 | tf_op jit(solution)/shard_map/ppermute | solution.py:227
  22.8 0.0 collective-permute-done.3.refs_3_
  22.8 1.5 %partial_sums.1 = (bf16[32,8,320]{2,1,0:T(8,128)(2,1)}, f32[160,1]{1,0:T(8,128)S(1)}) custom-call(bf16[36,2560]{1,0:T(8,128)(2,1)S(1)} %get-tuple-element.19.refs_0_, bf16[36,2560]{1,0:T(8,128)(2,1)S(1)} %collective-permute-done.1.refs_1_, bf16[36,2560]{1,0:T(8,128)(2,1)S(1)} %collective-permute-done.2.refs_2_, ...), custom_call_target="tpu_custom_call" | custom-call | flops 52428800 | bytes 819200 | tf_op jit(solution)/shard_map/partial_sums/pallas_call | solution.py:257
  24.3 6.8 %all-to-all-start = ((bf16[32,8,320]{2,1,0:T(8,128)(2,1)}), bf16[32,8,320]{2,1,0:T(8,128)(2,1)S(1)}, u32[]{:S(2)}, u32[]{:S(2)}) async-start(bf16[32,8,320]{2,1,0:T(8,128)(2,1)} %get-tuple-element.15), calls=%async_computation | async-start | bytes 393216 | tf_op jit(solution)/shard_map/all_to_all | solution.py:269
  31.2 0.0 copy-start.1
  31.2 1.8 %collective-permute-start = (bf16[1,128,1024]{2,1,0:T(8,128)(2,1)S(1)}, bf16[1,128,1024]{2,1,0:T(8,128)(2,1)S(1)}, u32[]{:S(2)}, u32[]{:S(2)}) collective-permute-start(bf16[1,128,1024]{2,1,0:T(8,128)(2,1)S(1)} %pad_maximum_fusion), channel_id=1, source_target_pairs={{0,4},{4,0},{1,5},{5,1},{2,6},{6,2},{3,7},{7,3},{8,12},{12,8},{9,1... | collective-permute-start | bytes 786440 | tf_op jit(solution)/shard_map/ppermute | solution.py:97
  33.1 1.7 %token_outputs.1 = (bf16[128,2560]{1,0:T(8,128)(2,1)}, f32[1,128]{1,0:T(1,128)}) custom-call(s32[1,128]{1,0:T(1,128)S(1)} %bitcast.13, s32[1,128]{1,0:T(1,128)S(1)} %bitcast.15, f32[1,128]{1,0:T(1,128)S(1)} %bitcast.17, f32[160,1]{1,0:T(8,128)S(1)} %get-tuple-element.12.inner_ref, bf16[36,2560]{1,0:T(8,128)(2,1)S(1)} %get-tuple-element.19.refs_0_, ...), custom_call_target="tpu_custom_call" | custom-call | flops 104857600 | bytes 1310720 | tf_op jit(solution)/shard_map/token_outputs/pallas_call | solution.py:277
  34.8 6.9 %collective-permute-done.refs_2_.refs_3_ = bf16[1,128,1024]{2,1,0:T(8,128)(2,1)S(1)} collective-permute-done((bf16[1,128,1024]{2,1,0:T(8,128)(2,1)S(1)}, bf16[1,128,1024]{2,1,0:T(8,128)(2,1)S(1)}, u32[]{:S(2)}, u32[]{:S(2)}) %collective-permute-start) | collective-permute-done | bytes 262176 | tf_op jit(solution)/shard_map/ppermute | solution.py:97
  41.7 0.0 copy-done.1
  41.7 6.7 %attend.1 = bf16[1,128,2560]{2,1,0:T(8,128)(2,1)} custom-call(bf16[1,128,2560]{2,1,0:T(8,128)(2,1)S(1)} %copy-done.1, bf16[1,128,512]{2,1,0:T(8,128)(2,1)S(1)} %copy-done.2, bf16[1,128,512]{2,1,0:T(8,128)(2,1)S(1)} %copy-done.3, bf16[1,128,1024]{2,1,0:T(8,128)(2,1)S(1)} %collective-permute-done.refs_2_.refs_3_, ...), custom_call_target="tpu_custom_call" | custom-call | flops 335544320 | bytes 1310720 | tf_op jit(solution)/shard_map/attend/pallas_call | solution.py:104
  48.4 0.0 all-to-all-done
  48.4 0.6 %convert_reduce_fusion = f32[8,320]{1,0:T(8,128)} fusion(bf16[32,8,320]{2,1,0:T(8,128)(2,1)S(1)} %all-to-all-done), kind=kLoop, calls=%fused_computation | loop fusion | flops 161280 | bytes 174080 | tf_op jit(solution)/shard_map/reduce_sum | solution.py:272
  (8 shorter events, 0.0 us)
Async XLA Ops:
  1.9 5.8 %copy-start = (bf16[128,2560]{1,0:T(8,128)(2,1)S(1)}, bf16[128,2560]{1,0:T(8,128)(2,1)}, u32[]{:S(2)}) copy-start(bf16[128,2560]{1,0:T(8,128)(2,1)} %feature_ref.1) | copy-start | bytes 1966084
  2.0 11.8 %collective-permute-start.1 = (bf16[36,2560]{1,0:T(8,128)(2,1)S(1)}, bf16[36,2560]{1,0:T(8,128)(2,1)S(1)}, u32[]{:S(2)}, u32[]{:S(2)}) collective-permute-start(bf16[36,2560]{1,0:T(8,128)(2,1)S(1)} %get-tuple-element.18), channel_id=1, source_target_pairs={{0,1},{1,0},{2,3},{3,2},{4,5},{5,4},{6,7},{7,6},{8,9},{9,8},{10,11... | collective-permute-start | bytes 552968 | tf_op jit(solution)/shard_map/ppermute | solution.py:227
  5.2 17.6 %collective-permute-start.2 = (bf16[36,2560]{1,0:T(8,128)(2,1)S(1)}, bf16[36,2560]{1,0:T(8,128)(2,1)S(1)}, u32[]{:S(2)}, u32[]{:S(2)}) collective-permute-start(bf16[36,2560]{1,0:T(8,128)(2,1)S(1)} %get-tuple-element.17), channel_id=1, source_target_pairs={{0,2},{1,3},{2,0},{3,1},{4,6},{5,7},{6,4},{7,5},{8,10},{9,11},{10,... | collective-permute-start | bytes 552968 | tf_op jit(solution)/shard_map/ppermute | solution.py:227
  7.7 15.0 %collective-permute-start.3 = (bf16[36,2560]{1,0:T(8,128)(2,1)S(1)}, bf16[36,2560]{1,0:T(8,128)(2,1)S(1)}, u32[]{:S(2)}, u32[]{:S(2)}) collective-permute-start(bf16[36,2560]{1,0:T(8,128)(2,1)S(1)} %get-tuple-element.16), channel_id=1, source_target_pairs={{0,3},{1,2},{2,1},{3,0},{4,7},{5,6},{6,5},{7,4},{8,11},{9,10},{10,... | collective-permute-start | bytes 552968 | tf_op jit(solution)/shard_map/ppermute | solution.py:227
  7.7 0.7 %copy-start.4 = (s32[128]{0:T(128)S(1)}, s32[128]{0:T(128)}, u32[]{:S(2)}) copy-start(s32[128]{0:T(128)} %param.13) | copy-start | bytes 1540
  7.7 0.7 %copy-start.5 = (s32[128]{0:T(128)S(1)}, s32[128]{0:T(128)}, u32[]{:S(2)}) copy-start(s32[128]{0:T(128)} %param.14) | copy-start | bytes 1540
  7.8 0.7 %copy-start.6 = (f32[128]{0:T(128)S(1)}, f32[128]{0:T(128)}, u32[]{:S(2)}) copy-start(f32[128]{0:T(128)} %param.12) | copy-start | bytes 1540
  24.3 6.9 %copy-start.2 = (bf16[1,128,512]{2,1,0:T(8,128)(2,1)S(1)}, bf16[1,128,512]{2,1,0:T(8,128)(2,1)}, u32[]{:S(2)}) copy-start(bf16[1,128,512]{2,1,0:T(8,128)(2,1)} %refs_0_.1) | copy-start | bytes 393220
  24.3 6.9 %copy-start.3 = (bf16[1,128,512]{2,1,0:T(8,128)(2,1)S(1)}, bf16[1,128,512]{2,1,0:T(8,128)(2,1)}, u32[]{:S(2)}) copy-start(bf16[1,128,512]{2,1,0:T(8,128)(2,1)} %refs_1_.1) | copy-start | bytes 393220
  24.3 24.1 %all-to-all-start = ((bf16[32,8,320]{2,1,0:T(8,128)(2,1)}), bf16[32,8,320]{2,1,0:T(8,128)(2,1)S(1)}, u32[]{:S(2)}, u32[]{:S(2)}) async-start(bf16[32,8,320]{2,1,0:T(8,128)(2,1)} %get-tuple-element.15), calls=%async_computation | async-start | bytes 393216 | tf_op jit(solution)/shard_map/all_to_all | solution.py:269
  31.2 10.5 %copy-start.1 = (bf16[1,128,2560]{2,1,0:T(8,128)(2,1)S(1)}, bf16[1,128,2560]{2,1,0:T(8,128)(2,1)}, u32[]{:S(2)}) copy-start(bf16[1,128,2560]{2,1,0:T(8,128)(2,1)} %q_ref.1) | copy-start | bytes 1966084
  31.2 10.5 %collective-permute-start = (bf16[1,128,1024]{2,1,0:T(8,128)(2,1)S(1)}, bf16[1,128,1024]{2,1,0:T(8,128)(2,1)S(1)}, u32[]{:S(2)}, u32[]{:S(2)}) collective-permute-start(bf16[1,128,1024]{2,1,0:T(8,128)(2,1)S(1)} %pad_maximum_fusion), channel_id=1, source_target_pairs={{0,4},{4,0},{1,5},{5,1},{2,6},{6,2},{3,7},{7,3},{8,12},{12,8},{9,1... | collective-permute-start | bytes 786440 | tf_op jit(solution)/shard_map/ppermute | solution.py:97
